TPU v7x, 128 devices: a whole 4x4x4 slice. The times are simulated.
128 devices in a mesh: row: 16 (over y_hi, z, core), col: 8 (over y_lo, x).
Axes of the slice: x: 4, y: 4 (y_hi: 2, y_lo: 2; y = y_hi * 2 + y_lo), z: 4, core: 2. Of those that a mesh axis runs over, the one named last changes fastest.
Arguments:
- gate_input: bfloat16 [2, 1024, 53248], P(None, 'col', 'row'), may hold values from -6 to 6
- up_input: bfloat16 [2, 1024, 53248], P(None, 'col', 'row'), may hold values from -6 to 6
- down_weight: bfloat16 [53248, 16384], P('row', 'col'), may hold values from -0.02734375 to 0.02734375
Outputs:
- mixed: bfloat16 [2, 1024, 16384], P(None, 'row', 'col')
All inputs are finite; a program needn't handle non-finite values.
Results may differ from a plain program's by a relative error of at most 0.0049.
Values may be sent and summed in bfloat16 or wider, within the bound.
A program may use at most 128 MiB of HBM per device.

v0:
```python
import jax
import jax.numpy as jnp
from jax import lax
from jax.sharding import PartitionSpec as P


def gated_hidden(gate_part, up_part):
    product = jax.nn.silu(gate_part.astype(jnp.float32)) * up_part.astype(jnp.float32)
    return product.astype(jnp.bfloat16)


def gathered_hidden(gate_part, up_part):
    return lax.all_gather(gated_hidden(gate_part, up_part), "col", axis=1, tiled=True)


def body(gate_input, up_input, down_weight):
    hidden_units = down_weight.shape[0]
    width = down_weight.shape[1]
    hidden = gathered_hidden(gate_input, up_input)
    seq_count = hidden.shape[0]
    seq_tokens = hidden.shape[1]
    flat = hidden.reshape(seq_count * seq_tokens, hidden_units)
    partial_value = jnp.dot(flat, down_weight, preferred_element_type=jnp.float32)
    partial_value = partial_value.reshape(seq_count, seq_tokens, width)
    mixed = lax.psum_scatter(partial_value, "row", scatter_dimension=1, tiled=True)
    return mixed.astype(jnp.bfloat16)


def solution(mesh):
    return jax.shard_map(
        body,
        mesh=mesh,
        in_specs=(P(None, "col", "row"), P(None, "col", "row"), P("row", "col")),
        out_specs=P(None, "row", "col"),
        check_vma=False,
    )
```

profile of v0, /device:TPU:0, one launch (start us, length us, event | category | flops | bytes accessed | tf_op | source)
XLA Modules:
  0.0 345.1 jit_solution(2053406622738443245)
XLA Ops:
  6.5 0.0 all-gather.2.cloned.1.call-start
  6.5 4.2 %fusion.6 = bf16[2,128,3328]{2,1,0:T(8,128)(2,1)} fusion(bf16[2,128,3328]{2,1,0:T(8,128)(2,1)} %param.4, bf16[2,128,3328]{2,1,0:T(8,128)(2,1)} %param.3), kind=kLoop, calls=%fused_computation.8 | loop fusion | flops 6815744 | bytes 5111808 | tf_op jit(solution)/shard_map/convert_element_type | solution.py:9
  10.7 0.0 all-gather.2.cloned.1.call-update
  10.7 0.0 reduce-scatter.2.cloned.1.call-start
  10.8 143.6 %all-gather.2.cloned.1.call-done = bf16[2,1024,3328]{2,1,0:T(8,128)(2,1)} async-done(((bf16[2,128,3328]{2,1,0:T(8,128)(2,1)}), bf16[2,1024,3328]{2,1,0:T(8,128)(2,1)}) %all-gather.2.cloned.1.call-update) | async-done | bytes 13631504 | tf_op jit(solution)/shard_map/all_gather | solution.py:13
  154.4 35.6 %fusion = f32[2,1024,2048]{2,1,0:T(8,128)} fusion(bf16[2,1024,3328]{2,1,0:T(8,128)(2,1)} %all-gather.2.cloned.1.call-done, bf16[3328,2048]{1,0:T(8,128)(2,1)} %param.5), kind=kOutput, calls=%fused_computation | convolution fusion | flops 27917287424 | bytes 44040192 | tf_op jit(solution)/shard_map/dot_general | solution.py:23
  190.0 0.0 reduce-scatter.2.cloned.1.call-update
  190.0 146.2 %reduce-scatter.2.cloned.1.call-done = f32[2,64,2048]{2,1,0:T(8,128)} async-done(((f32[2,1024,2048]{2,1,0:T(8,128)}), f32[2,64,2048]{2,1,0:T(8,128)}) %reduce-scatter.2.cloned.1.call-update) | async-done | bytes 1048592 | tf_op jit(solution)/shard_map/reduce_scatter | solution.py:25
  336.2 2.1 convert_element_type.15
Async XLA Ops:
  6.5 147.8 %all-gather.2.cloned.1.call-start = ((), (), s32[]{:S(2)}) async-start(), calls=%async_computation.1 | async-start | bytes 15335424 | tf_op jit(solution)/shard_map/all_gather | solution.py:13
  10.7 325.5 %reduce-scatter.2.cloned.1.call-start = ((), (), s32[]{:S(2)}) async-start(), calls=%async_computation.2 | async-start | bytes 17825792 | tf_op jit(solution)/shard_map/reduce_scatter | solution.py:25
Sparse Core Ops, SparseCore 0:
  10.9 143.4 all-gather.1
  190.1 146.0 reduce-scatter.1
where the time goes:
time: 345 us
  waiting for transfers between devices  290 us (84%)
  matrix products  35.6 us (10%)
  between operations  13.4 us (4%)
  other arithmetic  6.26 us (2%)
    reduce_scatter x1, waiting for transfers between devices, body(): lax.psum_scatter(partial_value, 'row', scatter_dimension=1, tiled=True)  146 us
    all_gather x1, waiting for transfers between devices, gathered_hidden(): lax.all_gather(gated_hidden(gate_part, up_part), 'col', axis=1, tiled=True)  144 us
    dot_general x1, matrix products, body(): jnp.dot(flat, down_weight, preferred_element_type=jnp.float32)  35.6 us
  transfers between devices with their start and end apart: 2, of which 2 were waited for; matrix products, arithmetic and copies ran while one was open for 0% of the time, Pallas kernels for 0%

commit v1 on v0

--- a/solution.py
+++ b/solution.py
@@ -10,7 +10,12 @@
 
 
 def gathered_hidden(gate_part, up_part):
-    return lax.all_gather(gated_hidden(gate_part, up_part), "col", axis=1, tiled=True)
+    return jnp.concatenate(
+        lax.all_to_all(
+            jnp.stack([gated_hidden(gate_part, up_part)] * lax.axis_size("col")), "col", 0, 0
+        ),
+        axis=1,
+    )
 
 
 def body(gate_input, up_input, down_weight):

time: 345 us -> 366 us (1.061)
  blocking collectives: 0 us -> 158 us
  waiting for transfers between devices: 290 us -> 148 us
  local copies, waits for them, and re-layouts: 0 us -> 8.27 us
    all_to_all x0 -> x1, blocking collectives: none -> 158 us  [gathered_hidden(): lax.all_to_all(jnp.stack([gated_hidden(gate_part, up_part)] * lax.axis_si...]
    all_gather x1 -> x0, waiting for transfers between devices: 144 us -> none  [gathered_hidden(): lax.all_gather(gated_hidden(gate_part, up_part), 'col', axis=1, tiled=True)]
    another operation x0 -> x1, local copies, waits for them, and re-layouts: none -> 6.2 us  [gathered_hidden(): jnp.stack([gated_hidden(gate_part, up_part)] * lax.axis_size('col'))]
  transfers between devices with their start and end apart: 2 -> 1, of which waited for: 2 -> 1; matrix products, arithmetic and copies ran while one was open for 0% -> 0% of each run, Pallas kernels for 0% -> 0%
where the time goes in v1:
time: 366 us
  blocking collectives  158 us (43%)
  waiting for transfers between devices  148 us (40%)
  matrix products  33.6 us (9%)
  between operations  13.4 us (4%)
  local copies, waits for them, and re-layouts  8.27 us (2%)
  other arithmetic  5.06 us (1%)
    all_to_all x1, blocking collectives, gathered_hidden(): lax.all_to_all(jnp.stack([gated_hidden(gate_part, up_part)] * lax.axis_si...  158 us
    reduce_scatter x1, waiting for transfers between devices, body(): lax.psum_scatter(partial_value, 'row', scatter_dimension=1, tiled=True)  148 us
    dot_general x1, matrix products, body(): jnp.dot(flat, down_weight, preferred_element_type=jnp.float32)  33.6 us
  transfers between devices with their start and end apart: 1, of which 1 were waited for; matrix products, arithmetic and copies ran while one was open for 0% of the time, Pallas kernels for 0%

profile of v1, /device:TPU:0, one launch (start us, length us, event | category | flops | bytes accessed | tf_op | source)
XLA Modules:
  0.0 366.0 jit_solution(1355126779133044847)
XLA Ops:
  6.5 0.0 reduce-scatter.2.cloned.1.call-start
  6.5 3.0 fusion.6
  9.5 6.2 %stack.2 = bf16[8,2,128,3328]{3,2,1,0:T(8,128)(2,1)} broadcast(bf16[2,128,3328]{2,1,0:T(8,128)(2,1)S(1)} %fusion.6), dimensions={1,2,3} | broadcast | bytes 15335424 | tf_op jit(solution)/shard_map/stack | solution.py:15
  15.7 157.7 %all_to_all.5 = bf16[8,2,128,3328]{3,2,1,0:T(8,128)(2,1)S(1)} all-to-all(bf16[8,2,128,3328]{3,2,1,0:T(8,128)(2,1)} %stack.2), channel_id=1, replica_groups=mesh['row'=16,'col'=8] {'col'}, dimensions={0} | all-to-all | bytes 27262976 | tf_op jit(solution)/shard_map/all_to_all | solution.py:14
  173.4 2.1 copy.4
  175.5 33.6 %fusion = f32[2,1024,2048]{2,1,0:T(8,128)} fusion(bf16[2,1024,3328]{2,1,0:T(8,128)(2,1)S(1)} %bitcast.7, bf16[3328,2048]{1,0:T(8,128)(2,1)} %param.5), kind=kOutput, calls=%fused_computation | convolution fusion | flops 27917287424 | bytes 44040192 | tf_op jit(solution)/shard_map/dot_general | solution.py:28
  209.0 0.0 reduce-scatter.2.cloned.1.call-update
  209.1 148.0 %reduce-scatter.2.cloned.1.call-done = f32[2,64,2048]{2,1,0:T(8,128)} async-done(((f32[2,1024,2048]{2,1,0:T(8,128)}), f32[2,64,2048]{2,1,0:T(8,128)}) %reduce-scatter.2.cloned.1.call-update) | async-done | bytes 1048592 | tf_op jit(solution)/shard_map/reduce_scatter | solution.py:30
  357.1 2.1 convert_element_type.15
Async XLA Ops:
  6.5 350.6 %reduce-scatter.2.cloned.1.call-start = ((), (), s32[]{:S(2)}) async-start(), calls=%async_computation.2 | async-start | bytes 17825792 | tf_op jit(solution)/shard_map/reduce_scatter | solution.py:30
Sparse Core Ops, SparseCore 0:
  209.2 147.8 reduce-scatter.1
